TPU v7x, 1024 devices: a whole 4x4x32 slice. The times are simulated.
1024 devices in a mesh: dp: 16 (over y_hi, x, core), mp: 64 (over y_lo, z).
Axes of the slice: x: 4, y: 4 (y_hi: 2, y_lo: 2; y = y_hi * 2 + y_lo), z: 32, core: 2. Of those that a mesh axis runs over, the one named last changes fastest.
Arguments:
- tokens: bfloat16 [12288, 6144], P('dp'), may hold values from -60 to 60
- ln_gain: float32 [6144], replicated, may hold values from 0.1 to 1.9
- w_qkv: bfloat16 [6144, 3, 6144], P('dp', None, 'mp'), may hold values from -1 to 1
- q_gain: float32 [128], replicated, may hold values from 0.7 to 2
- k_gain: float32 [128], replicated, may hold values from 0.7 to 2
Outputs:
- context: bfloat16 [12288, 6144], P('dp', 'mp')
All inputs are finite; a program needn't handle non-finite values.
Results may differ from a plain program's by a relative error of at most 0.012.
The roundings to bfloat16 on the way count: a program that leaves them out, or rounds other values in their place, can miss the bound.
Values may be sent and summed in bfloat16 or wider, within the bound.
A program may use at most 64 MiB of HBM per device.

v0:
```python
import jax
import jax.numpy as jnp
from jax import lax
from jax.sharding import PartitionSpec as P

HEADS = 48
HEAD_DIM = 128
PATCHES = 256
SPLITS = 4


norm_eps = 1e-06


def partner(value, axis, distance):
    mask = 2**distance
    pairs = [(source, source ^ mask) for source in range(lax.axis_size(axis))]
    return lax.ppermute(value, axis, pairs)


def layer_norm(values, gain_vector):
    centre = jnp.mean(values, axis=-1, keepdims=True)
    centred = values - centre
    spread = jnp.mean(centred * centred, axis=-1, keepdims=True)
    return centred * lax.rsqrt(spread + norm_eps) * gain_vector


def head_norm(pieces, gain_rows):
    values = pieces.astype(jnp.float32)
    centre = jnp.mean(values, axis=(0, 4), keepdims=True)
    centred = values - centre
    spread = jnp.mean(centred * centred, axis=(0, 4), keepdims=True)
    return centred * lax.rsqrt(spread + norm_eps) * gain_rows[:, None, None, None, :]


def ordered_gains(gain_vector, quarter_order):
    gain_table = gain_vector.reshape(SPLITS, -1)
    selector = (quarter_order[:, None] == jnp.arange(SPLITS, dtype=jnp.int32)[None, :]).astype(
        jnp.float32
    )
    return jnp.dot(selector, gain_table, precision=lax.Precision.HIGHEST)


def body(tokens, ln_gain, w_qkv, q_gain, k_gain):
    local_rows = tokens.shape[0]
    normed = layer_norm(tokens.astype(jnp.float32), ln_gain).astype(jnp.bfloat16)
    flat_weight = w_qkv.reshape(w_qkv.shape[0], -1)
    out_width = flat_weight.shape[1]
    row_piece = lax.all_gather(w_qkv, "dp", axis=0, tiled=True)
    partial_value = jnp.dot(
        normed, row_piece.reshape(row_piece.shape[0], out_width), preferred_element_type=jnp.float32
    )
    projected = partial_value.astype(jnp.bfloat16)
    groups = lax.axis_size("mp") // SPLITS
    head_count = HEADS // groups
    my_quarter = lax.axis_index("mp") // groups
    images = local_rows // PATCHES
    head_view = projected.reshape(images, PATCHES, 3, head_count, HEAD_DIM // SPLITS)
    queries = head_view[:, :, 0]
    keys_vals = head_view[:, :, 1:]
    counting = jnp.arange(SPLITS, dtype=jnp.int32)
    query_pieces = queries[None]
    pair_pieces = keys_vals[None]
    low_bit = groups.bit_length() - 1
    for doubling in range(SPLITS.bit_length() - 1):
        got_query, got_pair = partner((query_pieces, pair_pieces), "mp", low_bit + doubling)
        query_pieces = jnp.concatenate([query_pieces, got_query], 0)
        pair_pieces = jnp.concatenate([pair_pieces, got_pair], 0)
    quarter_order = jnp.bitwise_xor(my_quarter, counting)
    query_normed = (
        head_norm(query_pieces, ordered_gains(q_gain, quarter_order)) * HEAD_DIM ** (-0.5)
    ).astype(jnp.bfloat16)
    key_normed = head_norm(pair_pieces[:, :, :, 0], ordered_gains(k_gain, quarter_order)).astype(
        jnp.bfloat16
    )
    value_part = pair_pieces[:, :, :, 1]
    scores = jnp.einsum(
        "sirhe,sikhe->ihrk", query_normed, key_normed, preferred_element_type=jnp.float32
    )
    raised = jnp.exp(scores)
    weights = (raised / jnp.sum(raised, axis=-1, keepdims=True)).astype(jnp.bfloat16)
    context = jnp.einsum(
        "ihrk,sikhe->sirhe", weights, value_part, preferred_element_type=jnp.float32
    ).astype(jnp.bfloat16)
    own_block = context[0]
    return own_block.reshape(local_rows, -1)


def solution(mesh):
    return jax.shard_map(
        body,
        mesh=mesh,
        in_specs=(P("dp", None), P(), P("dp", None, "mp"), P(), P()),
        out_specs=P("dp", "mp"),
        check_vma=False,
    )
```

profile of v0, /device:TPU:32, one launch (start us, length us, event | category | flops | bytes accessed | tf_op | source)
XLA Modules:
  0.0 253.4 jit_solution(11184187370068173622)
XLA Ops:
  6.5 0.7 all-gather.2.cloned.1.call-update
  7.3 0.7 reshape.59
  8.0 0.7 reshape.60
  8.7 5.2 %convert_reduce_fusion = f32[768]{0:T(1024)S(1)} fusion(bf16[768,6144]{1,0:T(8,128)(2,1)} %param.5), kind=kLoop, calls=%fused_computation.1 | loop fusion | flops 9436416 | bytes 9440256 | tf_op jit(solution)/shard_map/reduce_sum | solution.py:22
  13.9 1.2 copy-done
  15.1 2.6 %fusion.2 = f32[768]{0:T(1024)S(1)} fusion(bf16[768,6144]{1,0:T(8,128)(2,1)S(1)} %copy-done, f32[768]{0:T(1024)S(1)} %broadcast_multiply_fusion.1), kind=kLoop, calls=%fused_computation.4 | loop fusion | flops 18873600 | bytes 9443328 | tf_op jit(solution)/shard_map/reduce_sum | solution.py:24
  17.7 92.6 %all-gather.2.cloned.1.call-done = bf16[6144,3,96]{0,2,1:T(8,128)(2,1)} async-done(((bf16[384,3,96]{0,2,1:T(8,128)(2,1)}), bf16[6144,3,96]{0,2,1:T(8,128)(2,1)}) %all-gather.2.cloned.1.call-update) | async-done | bytes 3538960 | tf_op jit(solution)/shard_map/all_gather | solution.py:49
  110.4 7.9 %fusion.17 = bf16[768,288]{0,1:T(8,128)(2,1)S(1)} fusion(bf16[6144,288]{0,1:T(8,128)(2,1)} %bitcast.57, bf16[768,6144]{1,0:T(8,128)(2,1)} %param.5, f32[6144]{0:T(1024)S(1)} %copy-done.1, f32[768]{0:T(1024)S(1)} %add_rsqrt_fusion.1, f32[768]{0:T(1024)S(1)} %broadcast_multiply_fusion.1), kind=kOutput, calls=%fused_computation.25 | convolution fusion | flops 2741723136 | bytes 13449216 | tf_op jit(solution)/shard_map/dot_general | solution.py:50
  118.5 22.3 %collective-permute-start.2 = (bf16[1,3,256,3,32]{2,1,4,3,0:T(4,128)(2,1)S(1)}, bf16[1,3,256,3,32]{2,1,4,3,0:T(4,128)(2,1)S(1)}, u32[]{:S(2)}, u32[]{:S(2)}) collective-permute-start(bf16[1,3,256,3,32]{2,1,4,3,0:T(4,128)(2,1)S(1)} %slice_bitcast_fusion.2), channel_id=1, source_target_pairs={{0,16},{1,17},{2,18},{3,19},{4,20},{5,21},{6,22},{7,23},{8,24},{9,... | collective-permute-start | bytes 442376 | tf_op jit(solution)/shard_map/ppermute | solution.py:18
  140.8 0.2 fusion.38
  141.1 1.9 collective-permute-start
  143.1 42.6 %collective-permute-done.2 = bf16[1,3,256,3,32]{2,1,4,3,0:T(4,128)(2,1)S(1)} collective-permute-done((bf16[1,3,256,3,32]{2,1,4,3,0:T(4,128)(2,1)S(1)}, bf16[1,3,256,3,32]{2,1,4,3,0:T(4,128)(2,1)S(1)}, u32[]{:S(2)}, u32[]{:S(2)}) %collective-permute-start.2) | collective-permute-done | bytes 147488 | tf_op jit(solution)/shard_map/ppermute | solution.py:18
  185.7 0.3 pad_maximum_fusion.3
  186.0 2.5 collective-permute-start.3
  188.7 38.7 %collective-permute-done = bf16[1,3,256,2,3,32]{2,5,0,4,1,3:T(8,128)(2,1)S(1)} collective-permute-done((bf16[1,3,256,2,3,32]{2,5,0,4,1,3:T(8,128)(2,1)S(1)}, bf16[1,3,256,2,3,32]{2,5,0,4,1,3:T(8,128)(2,1)S(1)}, u32[]{:S(2)}, u32[]{:S(2)}) %collective-permute-start) | collective-permute-done | bytes 294944 | tf_op jit(solution)/shard_map/ppermute | solution.py:18
  227.5 2.7 %collective-permute-start.1 = (bf16[2,3,256,2,3,32]{2,5,0,4,1,3:T(8,128)(2,1)S(1)}, bf16[2,3,256,2,3,32]{2,5,0,4,1,3:T(8,128)(2,1)S(1)}, u32[]{:S(2)}, u32[]{:S(2)}) collective-permute-start(bf16[2,3,256,2,3,32]{2,5,0,4,1,3:T(8,128)(2,1)S(1)} %pad_maximum_fusion.2), channel_id=1, source_target_pairs={{0,32},{1,33},{2,34},{3,35},{4,36},{5,37},{6,38},{7,39},{8,40},{9,... | collective-permute-start | bytes 1769480 | tf_op jit(solution)/shard_map/ppermute | solution.py:18
  230.2 0.5 convert_reduce_fusion.1
  230.7 0.5 fusion.13
  231.3 0.6 fusion.16
  231.9 12.2 %collective-permute-done.1 = bf16[2,3,256,2,3,32]{2,5,0,4,1,3:T(8,128)(2,1)S(1)} collective-permute-done((bf16[2,3,256,2,3,32]{2,5,0,4,1,3:T(8,128)(2,1)S(1)}, bf16[2,3,256,2,3,32]{2,5,0,4,1,3:T(8,128)(2,1)S(1)}, u32[]{:S(2)}, u32[]{:S(2)}) %collective-permute-start.1) | collective-permute-done | bytes 589856 | tf_op jit(solution)/shard_map/ppermute | solution.py:18
  244.3 0.2 fusion.24
  244.5 0.7 fusion.10
  245.2 0.5 fusion.20
  245.9 0.7 copy.34
  (24 shorter events, 1.1 us)
Async XLA Ops:
  6.5 103.8 %all-gather.2.cloned.1.call-start = ((), (), s32[]{:S(2)}) async-start(), calls=%async_computation | async-start | bytes 3760128 | tf_op jit(solution)/shard_map/all_gather | solution.py:49
  8.7 6.4 %copy-start = (bf16[768,6144]{1,0:T(8,128)(2,1)S(1)}, bf16[768,6144]{1,0:T(8,128)(2,1)}, u32[]{:S(2)}) copy-start(bf16[768,6144]{1,0:T(8,128)(2,1)} %param.5) | copy-start | bytes 28311556
  15.1 95.2 %copy-start.1 = (f32[6144]{0:T(1024)S(1)}, f32[6144]{0:T(1024)}, u32[]{:S(2)}) copy-start(f32[6144]{0:T(1024)} %param.6) | copy-start | bytes 73732
  118.5 67.2 %collective-permute-start.2 = (bf16[1,3,256,3,32]{2,1,4,3,0:T(4,128)(2,1)S(1)}, bf16[1,3,256,3,32]{2,1,4,3,0:T(4,128)(2,1)S(1)}, u32[]{:S(2)}, u32[]{:S(2)}) collective-permute-start(bf16[1,3,256,3,32]{2,1,4,3,0:T(4,128)(2,1)S(1)} %slice_bitcast_fusion.2), channel_id=1, source_target_pairs={{0,16},{1,17},{2,18},{3,19},{4,20},{5,21},{6,22},{7,23},{8,24},{9,... | collective-permute-start | bytes 442376 | tf_op jit(solution)/shard_map/ppermute | solution.py:18
  141.1 86.3 %collective-permute-start = (bf16[1,3,256,2,3,32]{2,5,0,4,1,3:T(8,128)(2,1)S(1)}, bf16[1,3,256,2,3,32]{2,5,0,4,1,3:T(8,128)(2,1)S(1)}, u32[]{:S(2)}, u32[]{:S(2)}) collective-permute-start(bf16[1,3,256,2,3,32]{2,5,0,4,1,3:T(8,128)(2,1)S(1)} %bitcast.53), channel_id=1, source_target_pairs={{0,16},{1,17},{2,18},{3,19},{4,20},{5,21},{6,22},{7,23},{8,24},{9,... | collective-permute-start | bytes 884744 | tf_op jit(solution)/shard_map/ppermute | solution.py:18
  186.0 44.2 %collective-permute-start.3 = (bf16[2,3,256,3,32]{2,1,4,3,0:T(4,128)(2,1)S(1)}, bf16[2,3,256,3,32]{2,1,4,3,0:T(4,128)(2,1)S(1)}, u32[]{:S(2)}, u32[]{:S(2)}) collective-permute-start(bf16[2,3,256,3,32]{2,1,4,3,0:T(4,128)(2,1)S(1)} %pad_maximum_fusion.3), channel_id=1, source_target_pairs={{0,32},{1,33},{2,34},{3,35},{4,36},{5,37},{6,38},{7,39},{8,40},{9,... | collective-permute-start | bytes 884744 | tf_op jit(solution)/shard_map/ppermute | solution.py:18
  227.5 16.6 %collective-permute-start.1 = (bf16[2,3,256,2,3,32]{2,5,0,4,1,3:T(8,128)(2,1)S(1)}, bf16[2,3,256,2,3,32]{2,5,0,4,1,3:T(8,128)(2,1)S(1)}, u32[]{:S(2)}, u32[]{:S(2)}) collective-permute-start(bf16[2,3,256,2,3,32]{2,5,0,4,1,3:T(8,128)(2,1)S(1)} %pad_maximum_fusion.2), channel_id=1, source_target_pairs={{0,32},{1,33},{2,34},{3,35},{4,36},{5,37},{6,38},{7,39},{8,40},{9,... | collective-permute-start | bytes 1769480 | tf_op jit(solution)/shard_map/ppermute | solution.py:18
Sparse Core Ops, SparseCore 0:
  11.6 98.6 all-gather.1
where the time goes:
time: 254 us; the launch traced here: 253 us
  waiting for transfers between devices  187 us (74%)
  starting transfers between devices  29.4 us (12%)
  between operations  13.6 us (5%)
  other arithmetic  10.2 us (4%)
  matrix products  9.42 us (4%)
  local copies, waits for them, and re-layouts  3.92 us (2%)
    ppermute x4, waiting for transfers between devices, partner(): return lax.ppermute(value, axis, pairs)  93.5 us
    all_gather x1, waiting for transfers between devices, body(): row_piece = lax.all_gather(w_qkv, 'dp', axis=0, tiled=True)  92.6 us
    ppermute x4, starting transfers between devices, partner(): return lax.ppermute(value, axis, pairs)  29.4 us
    dot_general x1, matrix products, body(): jnp.dot(normed, row_piece.reshape(row_piece.shape[0], out_width), preferr...  7.87 us
    reduce_sum x1, other arithmetic, layer_norm(): centre = jnp.mean(values, axis=-1, keepdims=True)  5.17 us
  transfers between devices with their start and end apart: 5, of which 4 were waited for; matrix products, arithmetic and copies ran while one was open for 5% of the time, Pallas kernels for 0%

commit v1 on v0

v1 whole, which is shorter than its diff:
```python
import functools

import jax
import jax.numpy as jnp
from jax import lax
from jax.experimental import pallas as pl
from jax.experimental.pallas import tpu as pltpu
from jax.sharding import PartitionSpec as P

HEADS = 48
HEAD_DIM = 128
PATCHES = 256
SPLITS = 4
EPS = 1e-06
MESH = pl.DeviceIdType.MESH
PART = HEAD_DIM // SPLITS
LOCAL_HEADS = 3
IMAGES = 3
ROWS = 768
WIDTH = 6144
DEPTH = 384
LN_ROWS = 16


def place():
    dp = lax.axis_index("dp")
    mp = lax.axis_index("mp")
    c = dp % 2
    x = (dp // 2) % 4
    y = (dp // 8) * 2 + mp // 32
    return y + c * (x - y), x + c * (y - x), c, mp % 32


def device(a, b, c, z):
    x = b + c * (a - b)
    y = a + c * (b - a)
    return ((y // 2) * 8 + x * 2 + c, (y % 2) * 32 + z)


def norm_rows(rows, xn, gain_ref):
    x = xn[rows, :].astype(jnp.float32)
    mean = jnp.sum(x, axis=1, keepdims=True) * (1.0 / WIDTH)
    centred = xn[rows, :].astype(jnp.float32) - mean
    spread = jnp.sum(centred * centred, axis=1, keepdims=True) * (1.0 / WIDTH)
    scale = lax.rsqrt(spread + EPS)
    centred = xn[rows, :].astype(jnp.float32) - mean
    xn[rows, :] = (centred * scale * gain_ref[...]).astype(jnp.bfloat16)


def head_norm(pieces, gain):
    values = pieces.astype(jnp.bfloat16).astype(jnp.float32)
    centred = values - jnp.mean(values, axis=1, keepdims=True)
    spread = jnp.mean(centred * centred, axis=1, keepdims=True)
    return centred * lax.rsqrt(spread + EPS) * gain


def gain_row(gain_ref, upper):
    g = [gain_ref[:, r * PART : (r + 1) * PART] for r in range(SPLITS)]
    pick = lambda one, other: jnp.where(upper == 0, one, other)
    return jnp.concatenate(
        [pick(g[0], g[1]), pick(g[2], g[3]), pick(g[1], g[0]), pick(g[3], g[2])], axis=1
    )


def kernel(
    tok_ref, gain_ref, w_ref, q_gain_ref, k_gain_ref, out_ref,
    xn, own, far, val, acc, vt,
    tok_sem, w_sem, z_send, z_recv, one_send, one_recv, two_send, two_recv,
    sib_send, sib_recv, v_send, v_recv, vs_send, vs_recv,
):
    a, b, c, z = place()
    x = b + c * (a - b)
    y = a + c * (b - a)
    yh, yl = y // 2, y % 2
    upper = z // 16
    z_peer = device(a, b, c, (z + 16) % 32)
    sibling = device(y + (1 - c) * (x - y), x + (1 - c) * (y - x), 1 - c, z)
    b_peers = [device(a, (b + j) % 4, c, z) for j in (1, 2, 3)]
    a_peers = [device((a + j) % 4, b, c, z) for j in (1, 2, 3)]
    v_shift = [(1, 0), (2, 0), (3, 0), (0, 2), (1, 2), (2, 2), (3, 2)]

    def v_peer(i, k):
        px, py = (x + i) % 4, (y + k) % 4
        return ((py // 2) * 8 + px * 2 + c, (py % 2) * 32 + z)

    barrier = pltpu.get_barrier_semaphore()
    peers = [z_peer, sibling] + b_peers + a_peers + [v_peer(i, 2) for i in (1, 2, 3)]
    for peer in peers:
        pl.semaphore_signal(barrier, inc=1, device_id=peer, device_id_type=MESH)

    tok_copies = [
        pltpu.make_async_copy(
            tok_ref.at[pl.ds(i * PATCHES, PATCHES)],
            xn.at[pl.ds(i * PATCHES, PATCHES)],
            tok_sem.at[i],
        )
        for i in range(IMAGES)
    ]
    w_copy = pltpu.make_async_copy(w_ref.at[pl.ds(0, 2)], own.at[c, a, b], w_sem.at[0])
    v_copy = pltpu.make_async_copy(w_ref.at[2], val.at[c, yh, x], w_sem.at[1])
    w_copy.start()
    v_copy.start()
    for copy in tok_copies:
        copy.start()

    def remote(src, dst, send, recv, peer):
        return pltpu.make_async_remote_copy(
            src_ref=src, dst_ref=dst, send_sem=send, recv_sem=recv, device_id=peer,
            device_id_type=MESH,
        )

    def same(ref, send, recv, peer):
        return remote(ref, ref, send, recv, peer)

    z_copies = [
        remote(own.at[c, a, b, :, h], far.at[h, c, a, b], z_send.at[h], z_recv.at[h], z_peer)
        for h in range(LOCAL_HEADS)
    ]

    def first(n, ref):
        return [same(ref, one_send.at[n, j], one_recv.at[n, j], b_peers[j]) for j in range(3)]

    def second(n, ref):
        return [same(ref, two_send.at[n, j], two_recv.at[n, j], a_peers[j]) for j in range(3)]

    own_one = first(3, own.at[c, a, b])
    own_two = second(3, own.at[c, a])
    own_sib = same(own.at[c], sib_send.at[3], sib_recv.at[3], sibling)
    far_one = [first(h, far.at[h, c, a, b]) for h in range(LOCAL_HEADS)]
    far_two = [second(h, far.at[h, c, a]) for h in range(LOCAL_HEADS)]
    far_sib = [
        same(far.at[h, c], sib_send.at[h], sib_recv.at[h], sibling) for h in range(LOCAL_HEADS)
    ]
    v_copies = [
        same(val.at[c, yh, x], v_send.at[n], v_recv.at[n], v_peer(i, k))
        for n, (i, k) in enumerate(v_shift)
    ]
    v_sib = same(val.at[c], vs_send, vs_recv, sibling)

    def start(copies):
        for copy in copies:
            copy.start()

    def arrived(copies):
        for copy in copies:
            copy.wait_recv()

    def left(copies):
        for copy in copies:
            copy.wait_send()

    for i in range(IMAGES):
        tok_copies[i].wait()

        def step(n, _):
            base = pl.multiple_of(i * PATCHES + n * LN_ROWS, LN_ROWS)
            norm_rows(pl.ds(base, LN_ROWS), xn, gain_ref)
            return 0

        lax.fori_loop(0, PATCHES // LN_ROWS, step, 0)

    w_copy.wait()
    v_copy.wait()
    pl.semaphore_wait(barrier, len(peers))
    start(z_copies)
    start(own_one)
    start(v_copies)
    arrived(own_one)
    start(own_two)

    def columns(n):
        return pl.ds(pl.multiple_of(n * 2 * DEPTH, 2 * DEPTH), 2 * DEPTH)

    dims = (((1,), (1,)), ((), ()))

    def project_values():
        acc[...] = jnp.zeros_like(acc)

        def step(n, _):
            rhs = jnp.concatenate([val[0, n // 4, n % 4], val[1, n // 4, n % 4]], axis=2)
            rhs = rhs.reshape(LOCAL_HEADS * PART, 2 * DEPTH)
            rhs = jnp.concatenate([rhs, jnp.zeros((PART, 2 * DEPTH), rhs.dtype)], axis=0)
            acc[:, :HEAD_DIM] += lax.dot_general(
                xn[:, columns(n)], rhs, dims, preferred_element_type=jnp.float32
            )
            return 0

        lax.fori_loop(0, 8, step, 0)
        vt[...] = acc[:, :HEAD_DIM].T.astype(jnp.bfloat16)

    def project_head(h):
        acc[...] = jnp.zeros_like(acc)

        def step(n, _):
            hi, col = n // 4, n % 4
            rows = []
            for t in range(2):
                for low in range(2):
                    rows.append(
                        jnp.concatenate(
                            [own[0, hi * 2 + low, col, t, h], own[1, col, hi * 2 + low, t, h]], axis=1
                        )
                    )
                for low in range(2):
                    rows.append(
                        jnp.concatenate(
                            [far[h, 0, hi * 2 + low, col, t], far[h, 1, col, hi * 2 + low, t]], axis=1
                        )
                    )
            rhs = jnp.concatenate(rows, axis=0)
            acc[...] += lax.dot_general(
                xn[:, columns(n)], rhs, dims, preferred_element_type=jnp.float32
            )
            return 0

        lax.fori_loop(0, 8, step, 0)

    q_gain = gain_row(q_gain_ref, upper)
    k_gain = gain_row(k_gain_ref, upper)

    def attend(h):
        for i in range(IMAGES):
            rows = pl.ds(i * PATCHES, PATCHES)
            qn = (head_norm(acc[rows, :HEAD_DIM], q_gain) * HEAD_DIM ** (-0.5)).astype(jnp.bfloat16)
            kn = head_norm(acc[rows, HEAD_DIM:], k_gain).astype(jnp.bfloat16)
            scores = lax.dot_general(kn, qn, dims, preferred_element_type=jnp.float32)
            raised = jnp.exp(scores)
            weights = (raised / jnp.sum(raised, axis=0, keepdims=True)).astype(jnp.bfloat16)
            out_ref[pl.ds(h * PART, PART), rows] = jnp.dot(
                vt[pl.ds(h * PART, PART), rows], weights, preferred_element_type=jnp.float32
            ).astype(jnp.bfloat16)

    arrived([z_copies[0]])
    start(far_one[0])
    arrived(own_two)
    own_sib.start()
    arrived(far_one[0])
    start(far_two[0])
    arrived(v_copies)
    v_sib.start()
    arrived([z_copies[1]])
    start(far_one[1])
    arrived(far_two[0])
    far_sib[0].start()
    arrived(far_one[1])
    start(far_two[1])
    arrived([v_sib, own_sib])
    project_values()
    arrived([z_copies[2]])
    start(far_one[2])
    arrived(far_two[1])
    far_sib[1].start()
    arrived(far_one[2])
    start(far_two[2])
    arrived([far_sib[0]])
    project_head(0)
    attend(0)
    arrived(far_two[2])
    far_sib[2].start()
    arrived([far_sib[1]])
    project_head(1)
    attend(1)
    arrived([far_sib[2]])
    project_head(2)
    attend(2)
    left(z_copies + own_one + own_two + [own_sib, v_sib] + v_copies + far_sib)
    for h in range(LOCAL_HEADS):
        left(far_one[h] + far_two[h])


def body(tokens, ln_gain, w_qkv, q_gain, k_gain):
    w = jnp.transpose(w_qkv, (1, 2, 0)).reshape(3, LOCAL_HEADS, PART, DEPTH)
    vmem = pl.BlockSpec(memory_space=pltpu.VMEM)
    hbm = pl.BlockSpec(memory_space=pl.ANY)
    dma = pltpu.SemaphoreType.DMA
    context = pl.pallas_call(
        kernel,
        out_shape=jax.ShapeDtypeStruct((LOCAL_HEADS * PART, ROWS), jnp.bfloat16),
        in_specs=[hbm, vmem, hbm, vmem, vmem],
        out_specs=vmem,
        scratch_shapes=[
            pltpu.VMEM((ROWS, WIDTH), jnp.bfloat16),
            pltpu.VMEM((2, 4, 4, 2, LOCAL_HEADS, PART, DEPTH), jnp.bfloat16),
            pltpu.VMEM((LOCAL_HEADS, 2, 4, 4, 2, PART, DEPTH), jnp.bfloat16),
            pltpu.VMEM((2, 2, 4, LOCAL_HEADS, PART, DEPTH), jnp.bfloat16),
            pltpu.VMEM((ROWS, 2 * HEAD_DIM), jnp.float32),
            pltpu.VMEM((HEAD_DIM, ROWS), jnp.bfloat16),
            dma((3,)), dma((2,)), dma((3,)), dma((3,)),
            dma((4, 3)), dma((4, 3)), dma((4, 3)), dma((4, 3)),
            dma((4,)), dma((4,)), dma((7,)), dma((7,)), dma, dma,
        ],
        compiler_params=pltpu.CompilerParams(
            collective_id=0, has_side_effects=True, vmem_limit_bytes=60 * 1024 * 1024
        ),
    )(tokens, ln_gain[None, :], w, q_gain[None, :], k_gain[None, :])
    return context.T


def solution(mesh):
    return jax.shard_map(
        body,
        mesh=mesh,
        in_specs=(P("dp", None), P(), P("dp", None, "mp"), P(), P()),
        out_specs=P("dp", "mp"),
        check_vma=False,
    )
```

time: 254 us -> 105 us (0.41)
  the two profiles are of different devices: /device:TPU:32 before, /device:TPU:160 now
where the time goes in v1:
time: 105 us
  Pallas kernels  103 us (98%)
  local copies, waits for them, and re-layouts  1.58 us (2%)
    pallas_call x1, Pallas kernels, body(): pl.pallas_call(kernel, out_shape=jax.ShapeDtypeStruct((LOCAL_HEADS * PART...  103 us

profile of v1, /device:TPU:160, one launch (start us, length us, event | category | flops | bytes accessed | tf_op | source)
XLA Modules:
  0.0 104.8 jit_solution(11794853216890637422)
XLA Ops:
  0.0 103.2 %shard_map.55 = bf16[96,768]{1,0:T(8,128)(2,1)} custom-call(bf16[768,6144]{1,0:T(8,128)(2,1)} %tok_ref.1, f32[1,6144]{1,0:T(1,128)} %bitcast.9, bf16[3,3,32,384]{3,2,1,0:T(8,128)(2,1)} %bitcast.8, f32[1,128]{1,0:T(1,128)} %bitcast.10, f32[1,128]{1,0:T(1,128)} %bitcast.11), custom_call_target="tpu_custom_call" | custom-call | tf_op jit(solution)/shard_map/pallas_call | solution.py:276
  103.2 1.6 %copy.7 = bf16[768,96]{0,1:T(8,128)(2,1)} copy(bf16[768,96]{0,1:T(8,128)(2,1)} %bitcast.7) | data formatting | bytes 294912

commit v2 on v0

v2 whole, which is shorter than its diff:
```python
import jax
import jax.numpy as jnp
from jax import lax
from jax.experimental import pallas as pl
from jax.experimental.pallas import tpu as pltpu
from jax.sharding import PartitionSpec as P

HEADS = 48
HEAD_DIM = 128
PATCHES = 256
SPLITS = 4
EPS = 1e-06
MESH = pl.DeviceIdType.MESH
PART = HEAD_DIM // SPLITS
HALF = HEAD_DIM // 2
LOCAL_HEADS = 3
IMAGES = 3
ROWS = 768
WIDTH = 6144
DEPTH = 384
LN_ROWS = 16
LN_SLICES = 4
LEG = 4
LEGS = 16 // LEG
COPIES = 128
CONTRACT_LAST = (((1,), (1,)), ((), ()))


def norm_rows(base, xn, gain_ref):
    rows = pl.ds(base, LN_ROWS)
    tiles = [pl.ds(128 * t, 128) for t in range(WIDTH // 128)]

    def load(tile):
        return xn[rows, tile].astype(jnp.float32)

    def row_mean(parts):
        total = (parts[0] + parts[1]) + (parts[2] + parts[3])
        return jnp.sum(total, axis=1, keepdims=True) * (1.0 / WIDTH)

    parts = [load(tile) for tile in tiles[:4]]
    for n, tile in enumerate(tiles[4:]):
        parts[n % 4] = parts[n % 4] + load(tile)
    mean = row_mean(parts)
    parts = [None] * 4
    for n, tile in enumerate(tiles):
        centred = load(tile) - mean
        square = centred * centred
        parts[n % 4] = square if n < 4 else parts[n % 4] + square
    scale = lax.rsqrt(row_mean(parts) + EPS)
    for tile in tiles:
        xn[rows, tile] = ((load(tile) - mean) * scale * gain_ref[:, tile]).astype(jnp.bfloat16)


def head_norm(values, gain):
    centred = values - jnp.mean(values, axis=1, keepdims=True)
    spread = jnp.mean(centred * centred, axis=1, keepdims=True)
    return centred * lax.rsqrt(spread + EPS) * gain


def gain_row(gain_ref, upper):
    g = [gain_ref[:, r * PART : (r + 1) * PART] for r in range(SPLITS)]
    pick = lambda one, other: jnp.where(upper == 0, one, other)
    return jnp.concatenate(
        [pick(g[0], g[1]), pick(g[2], g[3]), pick(g[1], g[0]), pick(g[3], g[2])], axis=1
    )


def kernel(
    tok_ref, gain_ref, w_ref, q_gain_ref, k_gain_ref, out_ref,
    xn, q_own, k_own, v_own, q_far, k_far, hop, acc, near, vt, give, take,
    tok_sem, w_sem, send_sem, recv_sem,
):
    dp = lax.axis_index("dp")
    mp = lax.axis_index("mp")
    c, x, yh = dp % 2, (dp // 2) % 4, dp // 8
    yl, z = mp // 32, mp % 32
    y = yh * 2 + yl
    upper = z // 16
    mine = 2 * yl
    other = 2 - 2 * yl
    pair = pl.ds(yl, 2)
    other_pair = pl.ds(1 - yl, 2)

    def device(px, py, pc, pz):
        return ((py // 2) * 8 + px * 2 + pc, (py % 2) * 32 + pz)

    def shifted(i, k):
        return device((x + i) % 4, (y + k) % 4, c, z)

    z_peers = [device(x, y, c, (z + LEG) % 32), device(x, y, c, (z + 32 - LEG) % 32)]
    sibling = device(x, y, 1 - c, z)
    partner = device(x, 2 * yh + 1 - yl, c, z)
    x_peers = [shifted(j, 0) for j in (1, 2, 3)]
    y_peers = [shifted(0, j) for j in (1, 2, 3)]
    shifts = [(i, k) for k in range(4) for i in range(4) if (i, k) != (0, 0)]

    barrier = pltpu.get_barrier_semaphore()
    peers = z_peers + [sibling] + [shifted(i, k) for i, k in shifts]
    for peer in peers:
        pl.semaphore_signal(barrier, inc=1, device_id=peer, device_id_type=MESH)

    w_copies = [
        pltpu.make_async_copy(w_ref.at[0], q_own.at[:, c, y, x], w_sem.at[0]),
        pltpu.make_async_copy(w_ref.at[1], k_own.at[:, c, y, x], w_sem.at[1]),
        pltpu.make_async_copy(w_ref.at[2], v_own.at[:, c, yl, yh, x], w_sem.at[2]),
    ]
    slice_rows = ROWS // LN_SLICES
    tok_copies = [
        pltpu.make_async_copy(
            tok_ref.at[pl.ds(i * slice_rows, slice_rows)],
            xn.at[pl.ds(i * slice_rows, slice_rows)],
            tok_sem.at[i],
        )
        for i in range(LN_SLICES)
    ]
    for copy in w_copies + tok_copies:
        copy.start()

    made = []

    def remote(src, dst, peer):
        n = len(made)
        made.append(
            pltpu.make_async_remote_copy(
                src_ref=src, dst_ref=dst, send_sem=send_sem.at[n], recv_sem=recv_sem.at[n],
                device_id=peer, device_id_type=MESH,
            )
        )
        return made[-1]

    def same(ref, peer):
        return remote(ref, ref, peer)

    def z_leg(leg, h):
        copies = []
        for way, (own, far) in enumerate(((q_own, q_far), (k_own, k_far))):
            src = own.at[h, c, y, x] if leg == 0 else hop.at[leg - 1, way, h]
            dst = far.at[h, c, y, x] if leg == LEGS - 1 else hop.at[leg, way, h]
            copies.append(remote(src, dst, z_peers[way]))
        return copies

    order = (0, 2, 1)
    z_copies = [{h: z_leg(leg, h) for h in order} for leg in range(LEGS)]
    to_y = [(other, other_pair), (mine, pair), (other, other_pair)]
    own_one = [same(q_own.at[:, c, y, x], peer) for peer in x_peers]
    own_one += [same(k_own.at[to_y[j][1], c, y, x], y_peers[j]) for j in range(3)]
    own_two = [same(q_own.at[to_y[j][1], c, y], y_peers[j]) for j in range(3)]
    own_two += [same(k_own.at[pair, c, :, x], peer) for peer in x_peers]
    own_sib = [same(q_own.at[pair, c], sibling), same(k_own.at[pair, c], sibling)]
    v_copies = [
        same(
            v_own.at[pair, c, yl, yh, x] if k % 2 == 0 else v_own.at[other, c, yl, yh, x],
            shifted(i, k),
        )
        for i, k in shifts
    ]
    v_sib = [same(v_own.at[mine, c], sibling), same(v_own.at[1, c, yl], sibling)]
    alone_one = [same(q_far.at[h, c, y, x], peer) for h in (0, 2) for peer in x_peers]
    alone_one += [same(k_far.at[to_y[j][0], c, y, x], y_peers[j]) for j in range(3)]
    alone_two = [same(q_far.at[to_y[j][0], c, y], y_peers[j]) for j in range(3)]
    alone_two += [same(k_far.at[mine, c, :, x], peer) for peer in x_peers]
    alone_sib = [same(q_far.at[mine, c], sibling), same(k_far.at[mine, c], sibling)]
    both_one = [same(q_far.at[1, c, y, x], peer) for peer in x_peers]
    both_one += [same(k_far.at[1, c, y, x], peer) for peer in y_peers]
    both_two = [same(q_far.at[1, c, y], peer) for peer in y_peers]
    both_two += [same(k_far.at[1, c, :, x], peer) for peer in x_peers]
    both_sib = [same(q_far.at[1, c], sibling), same(k_far.at[1, c], sibling)]
    back = remote(give, take, partner)

    def start(copies):
        for copy in copies:
            copy.start()

    def arrived(copies):
        for copy in copies:
            copy.wait_recv()

    def norm_slice(i):
        tok_copies[i].wait()

        def step(n, _):
            norm_rows(pl.multiple_of(i * slice_rows + n * LN_ROWS, LN_ROWS), xn, gain_ref)
            return 0

        lax.fori_loop(0, slice_rows // LN_ROWS, step, 0)

    def relay(leg):
        for h in order:
            for before, after in zip(z_copies[leg - 1][h], z_copies[leg][h]):
                before.wait_recv()
                after.start()

    def project(width, block):
        acc[:, :width] = jnp.zeros((ROWS, width), jnp.float32)

        def step(n, _):
            columns = pl.ds(pl.multiple_of(n * 2 * DEPTH, 2 * DEPTH), 2 * DEPTH)
            rows = [jnp.concatenate(halves, axis=1) for halves in block(n // 4, n % 4)]
            acc[:, :width] += lax.dot_general(
                xn[:, columns], jnp.concatenate(rows, axis=0), CONTRACT_LAST,
                preferred_element_type=jnp.float32,
            )
            return 0

        lax.fori_loop(0, 8, step, 0)

    def head_rows(queries, keys, h, hi, col):
        return [
            [ref[h, 0, hi * 2 + low, col], ref[h, 1, hi * 2 + low, col]]
            for ref in (queries, keys)
            for low in range(2)
        ]

    def project_near():
        project(
            2 * HEAD_DIM,
            lambda hi, col: head_rows(q_own, k_own, mine, hi, col)
            + head_rows(q_own, k_own, 1, hi, col),
        )
        near[...] = acc[...].astype(jnp.bfloat16)

    def project_values():
        def block(hi, col):
            rows = [[v_own[mine, half, low, hi, col] for half in range(2)] for low in (yl, 1 - yl)]
            rows.append([v_own[1, half, yl, hi, col] for half in range(2)])
            return rows + [[jnp.zeros((PART, DEPTH), jnp.bfloat16)] * 2]

        project(HEAD_DIM, block)
        vt[...] = acc[:, :HEAD_DIM].T.astype(jnp.bfloat16)

    def project_far(h):
        project(HEAD_DIM, lambda hi, col: head_rows(q_far, k_far, h, hi, col))

    q_gain = gain_row(q_gain_ref, upper)
    k_gain = gain_row(k_gain_ref, upper)

    def attend(slot, values):
        for i in range(IMAGES):
            rows = pl.ds(i * PATCHES, PATCHES)
            this = near[rows, pl.ds(slot * HEAD_DIM, HEAD_DIM)].astype(jnp.float32)
            that = acc[rows, :HEAD_DIM].astype(jnp.bfloat16).astype(jnp.float32)
            q = jnp.concatenate([this[:, :HALF], that[:, :HALF]], axis=1)
            k = jnp.concatenate([this[:, HALF:], that[:, HALF:]], axis=1)
            qn = (head_norm(q, q_gain) * HEAD_DIM ** (-0.5)).astype(jnp.bfloat16)
            kn = head_norm(k, k_gain).astype(jnp.bfloat16)
            scores = lax.dot_general(kn, qn, CONTRACT_LAST, preferred_element_type=jnp.float32)
            raised = jnp.exp(scores)
            weights = (raised / jnp.sum(raised, axis=0, keepdims=True)).astype(jnp.bfloat16)
            yield rows, jnp.dot(
                vt[values, rows], weights, preferred_element_type=jnp.float32
            ).astype(jnp.bfloat16)

    mine_rows = pl.ds(pl.multiple_of(mine * PART, PART), PART)
    other_rows = pl.ds(pl.multiple_of(other * PART, PART), PART)

    norm_slice(0)
    for copy in w_copies:
        copy.wait()
    pl.semaphore_wait(barrier, len(peers))
    for h in order:
        start(z_copies[0][h])
    start(own_one)
    norm_slice(1)
    relay(1)
    arrived(own_one)
    start(own_two)
    start(v_copies)
    norm_slice(2)
    relay(2)
    norm_slice(3)
    relay(3)
    arrived(own_two)
    start(own_sib)
    arrived(v_copies)
    start(v_sib)
    arrived(z_copies[-1][0] + z_copies[-1][2])
    start(alone_one)
    arrived(z_copies[-1][1])
    start(both_one)
    arrived(own_sib)
    project_near()
    arrived(alone_one)
    start(alone_two)
    arrived(both_one)
    start(both_two)
    arrived(v_sib)
    project_values()
    arrived(alone_two)
    start(alone_sib)
    arrived(alone_sib)
    project_far(mine)
    arrived(both_two)
    start(both_sib)
    for rows, result in attend(0, pl.ds(0, 2 * PART)):
        out_ref[mine_rows, rows] = result[:PART]
        give[:, rows] = result[PART:]
    arrived(both_sib)
    back.start()
    project_far(1)
    for rows, result in attend(1, pl.ds(2 * PART, PART)):
        out_ref[pl.ds(PART, PART), rows] = result
    back.wait_recv()
    out_ref[other_rows, :] = take[...]
    for copy in made:
        copy.wait_send()


def body(tokens, ln_gain, w_qkv, q_gain, k_gain):
    w = jnp.transpose(w_qkv, (1, 2, 0)).reshape(3, LOCAL_HEADS, PART, DEPTH)
    vmem = pl.BlockSpec(memory_space=pltpu.VMEM)
    hbm = pl.BlockSpec(memory_space=pl.ANY)
    dma = pltpu.SemaphoreType.DMA
    gathered = pltpu.VMEM((LOCAL_HEADS, 2, 4, 4, PART, DEPTH), jnp.bfloat16)
    context = pl.pallas_call(
        kernel,
        out_shape=jax.ShapeDtypeStruct((LOCAL_HEADS * PART, ROWS), jnp.bfloat16),
        in_specs=[hbm, vmem, hbm, vmem, vmem],
        out_specs=vmem,
        scratch_shapes=[
            pltpu.VMEM((ROWS, WIDTH), jnp.bfloat16),
            gathered,
            gathered,
            pltpu.VMEM((LOCAL_HEADS, 2, 2, 2, 4, PART, DEPTH), jnp.bfloat16),
            gathered,
            gathered,
            pltpu.VMEM((LEGS - 1, 2, LOCAL_HEADS, PART, DEPTH), jnp.bfloat16),
            pltpu.VMEM((ROWS, 2 * HEAD_DIM), jnp.float32),
            pltpu.VMEM((ROWS, 2 * HEAD_DIM), jnp.bfloat16),
            pltpu.VMEM((HEAD_DIM, ROWS), jnp.bfloat16),
            pltpu.VMEM((PART, ROWS), jnp.bfloat16),
            pltpu.VMEM((PART, ROWS), jnp.bfloat16),
            dma((LN_SLICES,)),
            dma((3,)),
            dma((COPIES,)),
            dma((COPIES,)),
        ],
        compiler_params=pltpu.CompilerParams(
            collective_id=0, has_side_effects=True, vmem_limit_bytes=60 * 1024 * 1024
        ),
    )(tokens, ln_gain[None, :], w, q_gain[None, :], k_gain[None, :])
    return context.T


def solution(mesh):
    return jax.shard_map(
        body,
        mesh=mesh,
        in_specs=(P("dp", None), P(), P("dp", None, "mp"), P(), P()),
        out_specs=P("dp", "mp"),
        check_vma=False,
    )
```

time: 254 us -> 86.5 us (0.34)
  the two profiles are of different devices: /device:TPU:32 before, /device:TPU:1 now
where the time goes in v2:
time: 86.5 us; the launch traced here: 86.3 us
  Pallas kernels  84.7 us (98%)
  local copies, waits for them, and re-layouts  1.58 us (2%)
    pallas_call x1, Pallas kernels, body(): pl.pallas_call(kernel, out_shape=jax.ShapeDtypeStruct((LOCAL_HEADS * PART...  84.7 us

profile of v2, /device:TPU:1, one launch (start us, length us, event | category | flops | bytes accessed | tf_op | source)
XLA Modules:
  0.0 86.3 jit_solution(16969300624820140950)
XLA Ops:
  0.0 84.7 %shard_map.55 = bf16[96,768]{1,0:T(8,128)(2,1)} custom-call(bf16[768,6144]{1,0:T(8,128)(2,1)} %tok_ref.1, f32[1,6144]{1,0:T(1,128)} %bitcast.9, bf16[3,3,32,384]{3,2,1,0:T(8,128)(2,1)} %bitcast.8, f32[1,128]{1,0:T(1,128)} %bitcast.10, f32[1,128]{1,0:T(1,128)} %bitcast.11), custom_call_target="tpu_custom_call" | custom-call | tf_op jit(solution)/shard_map/pallas_call | solution.py:314
  84.7 1.6 %copy.7 = bf16[768,96]{0,1:T(8,128)(2,1)} copy(bf16[768,96]{0,1:T(8,128)(2,1)} %bitcast.7) | data formatting | bytes 294912

commit v3 on v2

--- a/solution.py
+++ b/solution.py
@@ -138,6 +138,16 @@
             dst = far.at[h, c, y, x] if leg == LEGS - 1 else hop.at[leg, way, h]
             copies.append(remote(src, dst, z_peers[way]))
         return copies
+
+    def handed(h):
+        return [
+            copy
+            for j in range(4)
+            for copy in (
+                same(q_far.at[h, c, (y + 4 - j) % 4], sibling),
+                same(k_far.at[h, c, :, (x + 4 - j) % 4], sibling),
+            )
+        ]
 
     order = (0, 2, 1)
     z_copies = [{h: z_leg(leg, h) for h in order} for leg in range(LEGS)]
@@ -159,12 +169,12 @@
     alone_one += [same(k_far.at[to_y[j][0], c, y, x], y_peers[j]) for j in range(3)]
     alone_two = [same(q_far.at[to_y[j][0], c, y], y_peers[j]) for j in range(3)]
     alone_two += [same(k_far.at[mine, c, :, x], peer) for peer in x_peers]
-    alone_sib = [same(q_far.at[mine, c], sibling), same(k_far.at[mine, c], sibling)]
+    alone_sib = handed(mine)
     both_one = [same(q_far.at[1, c, y, x], peer) for peer in x_peers]
     both_one += [same(k_far.at[1, c, y, x], peer) for peer in y_peers]
     both_two = [same(q_far.at[1, c, y], peer) for peer in y_peers]
     both_two += [same(k_far.at[1, c, :, x], peer) for peer in x_peers]
-    both_sib = [same(q_far.at[1, c], sibling), same(k_far.at[1, c], sibling)]
+    both_sib = handed(1)
     back = remote(give, take, partner)
 
     def start(copies):
@@ -174,6 +184,11 @@
     def arrived(copies):
         for copy in copies:
             copy.wait_recv()
+
+    def hand_over(two, sib):
+        for j in range(3):
+            arrived([two[j], two[3 + j]])
+            start(sib[2 * j + 2 : 2 * j + 4])
 
     def norm_slice(i):
         tok_copies[i].wait()
@@ -194,15 +209,19 @@
         acc[:, :width] = jnp.zeros((ROWS, width), jnp.float32)
 
         def step(n, _):
-            columns = pl.ds(pl.multiple_of(n * 2 * DEPTH, 2 * DEPTH), 2 * DEPTH)
-            rows = [jnp.concatenate(halves, axis=1) for halves in block(n // 4, n % 4)]
+            columns = pl.ds(pl.multiple_of(n * 4 * DEPTH, 4 * DEPTH), 4 * DEPTH)
+            hi, col = n // 2, (n % 2) * 2
+            rows = [
+                jnp.concatenate(left + right, axis=1)
+                for left, right in zip(block(hi, col), block(hi, col + 1))
+            ]
             acc[:, :width] += lax.dot_general(
                 xn[:, columns], jnp.concatenate(rows, axis=0), CONTRACT_LAST,
                 preferred_element_type=jnp.float32,
             )
             return 0
 
-        lax.fori_loop(0, 8, step, 0)
+        lax.fori_loop(0, 4, step, 0)
 
     def head_rows(queries, keys, h, hi, col):
         return [
@@ -280,17 +299,15 @@
     arrived(own_sib)
     project_near()
     arrived(alone_one)
-    start(alone_two)
+    start(alone_two + alone_sib[:2])
     arrived(both_one)
-    start(both_two)
+    start(both_two + both_sib[:2])
     arrived(v_sib)
     project_values()
-    arrived(alone_two)
-    start(alone_sib)
+    hand_over(alone_two, alone_sib)
     arrived(alone_sib)
     project_far(mine)
-    arrived(both_two)
-    start(both_sib)
+    hand_over(both_two, both_sib)
     for rows, result in attend(0, pl.ds(0, 2 * PART)):
         out_ref[mine_rows, rows] = result[:PART]
         give[:, rows] = result[PART:]

time: 86.5 us -> 83.6 us (0.966)
  Pallas kernels: 84.7 us -> 81.8 us
    pallas_call x1, Pallas kernels: 84.7 us -> 81.8 us  [body(): pl.pallas_call(kernel, out_shape=jax.ShapeDtypeStruct((LOCAL_HEADS * PART...]
where the time goes in v3:
time: 83.6 us; the launch traced here: 83.4 us
  Pallas kernels  81.8 us (98%)
  local copies, waits for them, and re-layouts  1.58 us (2%)
    pallas_call x1, Pallas kernels, body(): pl.pallas_call(kernel, out_shape=jax.ShapeDtypeStruct((LOCAL_HEADS * PART...  81.8 us

profile of v3, /device:TPU:1, one launch (start us, length us, event | category | flops | bytes accessed | tf_op | source)
XLA Modules:
  0.0 83.4 jit_solution(55538277310770896)
XLA Ops:
  0.0 81.8 %shard_map.55 = bf16[96,768]{1,0:T(8,128)(2,1)} custom-call(bf16[768,6144]{1,0:T(8,128)(2,1)} %tok_ref.1, f32[1,6144]{1,0:T(1,128)} %bitcast.9, bf16[3,3,32,384]{3,2,1,0:T(8,128)(2,1)} %bitcast.8, f32[1,128]{1,0:T(1,128)} %bitcast.10, f32[1,128]{1,0:T(1,128)} %bitcast.11), custom_call_target="tpu_custom_call" | custom-call | tf_op jit(solution)/shard_map/pallas_call | solution.py:331
  81.8 1.6 %copy.7 = bf16[768,96]{0,1:T(8,128)(2,1)} copy(bf16[768,96]{0,1:T(8,128)(2,1)} %bitcast.7) | data formatting | bytes 294912
